TPU v7x, 512 devices: a whole 4x4x16 slice. The times are simulated.
512 devices in a mesh: dp: 16 (over z_lo, core), block: 32 (over y, z_hi, x).
Axes of the slice: x: 4, y: 4, z: 16 (z_hi: 2, z_lo: 8; z = z_hi * 8 + z_lo), core: 2. Of those that a mesh axis runs over, the one named last changes fastest.
Arguments:
- tokens: bfloat16 [4096, 16384], P('dp', 'block'), may hold values from -6 to 6
- upper_left: bfloat16 [64, 256, 1024], P('block', 'dp'), may hold values from -0.375 to 0.375
- upper_right: bfloat16 [256, 256, 256], P('block', 'dp'), may hold values from -0.375 to 0.375
- lower_right: bfloat16 [256, 256, 256], P('block', 'dp'), may hold values from -0.375 to 0.375
- lower_left: bfloat16 [64, 1024, 256], P('block', 'dp'), may hold values from -0.1875 to 0.1875
- cotangent: bfloat16 [4096, 16384], P('dp', 'block'), may hold values from -6 to 6
Outputs:
- output: bfloat16 [4096, 16384], P('dp', 'block')
- token_grad: bfloat16 [4096, 16384], P('dp', 'block')
- upper_left_grad: float32 [64, 256, 1024], P('block', 'dp')
- upper_right_grad: float32 [256, 256, 256], P('block', 'dp')
- lower_right_grad: float32 [256, 256, 256], P('block', 'dp')
- lower_left_grad: float32 [64, 1024, 256], P('block', 'dp')
All inputs are finite; a program needn't handle non-finite values.
Results may differ from a plain program's by a relative error of at most 0.017.
Values may be sent and summed in bfloat16 or wider, within the bound.
A program may use at most 64 MiB of HBM per device.

v0:
```python
import jax
import jax.numpy as jnp
from jax import lax
from jax.sharding import PartitionSpec as P


def contract(form, left, right):
    return jnp.einsum(form, left, right, preferred_element_type=jnp.float32)


def permute(values):
    return lax.all_to_all(values, "block", split_axis=1, concat_axis=0, tiled=True)


def forward(tokens, weights, mover):
    in_left, in_right, out_right, out_left = weights
    width = in_right.shape[1]
    rows = tokens.shape[0]
    local_blocks = in_left.shape[0]
    expand = in_left.shape[2] // width
    x_three = tokens.reshape(rows, local_blocks, width)
    left_four = in_left.reshape(local_blocks, width, expand, width)
    mixed = (
        contract("tkb,kbec->kect", x_three, left_four)
        .astype(jnp.bfloat16)
        .reshape(local_blocks * expand, width, rows)
    )
    spread = mover(mixed)
    hidden_pre = contract("act,cab->cbt", spread, in_right)
    active = jax.nn.gelu(hidden_pre).astype(jnp.bfloat16)
    narrow = contract("cbt,cbe->cet", active, out_right).astype(jnp.bfloat16)
    gathered = mover(narrow)
    narrow_four = gathered.reshape(width, local_blocks, expand, rows)
    out_four = out_left.reshape(local_blocks, expand, width, width)
    result = (
        contract("ckft,kfco->tko", narrow_four, out_four)
        .astype(jnp.bfloat16)
        .reshape(rows, local_blocks * width)
    )
    return (result, spread, hidden_pre, active, narrow_four)


def local(tokens, upper_left, upper_right, lower_right, lower_left, cotangent):
    weights = (
        lax.all_gather(upper_left, "dp", axis=1, tiled=True),
        lax.all_gather(upper_right, "dp", axis=1, tiled=True),
        lax.all_gather(lower_right, "dp", axis=1, tiled=True),
        lax.all_gather(lower_left, "dp", axis=1, tiled=True),
    )
    in_left, in_right, out_right, out_left = weights
    width = in_right.shape[1]
    rows = tokens.shape[0]
    local_blocks = in_left.shape[0]
    expand = in_left.shape[2] // width
    result, spread, hidden_pre, active, narrow_four = forward(tokens, weights, permute)
    x_three = tokens.reshape(rows, local_blocks, width)
    left_four = in_left.reshape(local_blocks, width, expand, width)
    out_four = out_left.reshape(local_blocks, expand, width, width)
    cot_three = cotangent.reshape(rows, local_blocks, width)
    grad_lower_left = contract("ckft,tko->kfco", narrow_four, cot_three).reshape(
        local_blocks, expand * width, width
    )
    back_narrow = (
        contract("tko,kfco->kfct", cot_three, out_four)
        .astype(jnp.bfloat16)
        .reshape(local_blocks * expand, width, rows)
    )
    narrow_back = permute(back_narrow)
    grad_lower_right = contract("cbt,ect->cbe", active, narrow_back)
    back_active = contract("ect,cbe->cbt", narrow_back, out_right)
    back_pre = jax.vjp(jax.nn.gelu, hidden_pre)[1](back_active)[0].astype(jnp.bfloat16)
    grad_upper_right = contract("act,cbt->cab", spread, back_pre)
    back_mixed = contract("cbt,cab->cat", back_pre, in_right).astype(jnp.bfloat16)
    mixed_back = permute(back_mixed).reshape(width, local_blocks, expand, rows)
    grad_upper_left = contract("tkb,cket->kbec", x_three, mixed_back).reshape(
        local_blocks, width, expand * width
    )
    token_grad = (
        contract("cket,kbec->tkb", mixed_back, left_four)
        .astype(jnp.bfloat16)
        .reshape(rows, local_blocks * width)
    )
    grad_upper_left, grad_upper_right, grad_lower_right, grad_lower_left = (
        lax.psum_scatter(
            grad_upper_left.astype(jnp.bfloat16), "dp", scatter_dimension=1, tiled=True
        ).astype(jnp.float32),
        lax.psum_scatter(
            grad_upper_right.astype(jnp.bfloat16), "dp", scatter_dimension=1, tiled=True
        ).astype(jnp.float32),
        lax.psum_scatter(
            grad_lower_right.astype(jnp.bfloat16), "dp", scatter_dimension=1, tiled=True
        ).astype(jnp.float32),
        lax.psum_scatter(
            grad_lower_left.astype(jnp.bfloat16), "dp", scatter_dimension=1, tiled=True
        ).astype(jnp.float32),
    )
    return (
        result,
        token_grad,
        grad_upper_left,
        grad_upper_right,
        grad_lower_right,
        grad_lower_left,
    )


def solution(mesh):
    in_specs = (
        P("dp", "block"),
        P("block", "dp", None),
        P("block", "dp", None),
        P("block", "dp", None),
        P("block", "dp", None),
        P("dp", "block"),
    )
    out_specs = (
        P("dp", "block"),
        P("dp", "block"),
        P("block", "dp", None),
        P("block", "dp", None),
        P("block", "dp", None),
        P("block", "dp", None),
    )
    return jax.shard_map(local, mesh=mesh, in_specs=in_specs, out_specs=out_specs, check_vma=False)
```

profile of v0, /device:TPU:6, one launch (start us, length us, event | category | flops | bytes accessed | tf_op | source)
XLA Modules:
  0.0 939.5 jit_solution(8600866587322765931)
XLA Ops:
  7.2 0.0 all-gather.5.cloned.1.call-start
  7.2 0.7 all-gather.5.cloned.1.call-update
  7.9 1.0 reshape.52
  8.9 104.0 %all-gather.5.cloned.1.call-done = bf16[2,256,1024]{2,1,0:T(8,128)(2,1)} async-done(((bf16[2,16,1024]{2,1,0:T(8,128)(2,1)}), bf16[2,256,1024]{2,1,0:T(8,128)(2,1)}) %all-gather.5.cloned.1.call-update) | async-done | bytes 1048592 | tf_op jit(solution)/shard_map/all_gather | solution.py:45
  112.9 1.5 copy.72
  114.4 0.5 convolution_convert_fusion.7
  114.8 0.0 copy-start.5
  114.8 1.6 copy.74
  116.4 18.3 %all-to-all-start = ((bf16[8,256,256]{2,0,1:T(8,128)(2,1)}), bf16[8,256,256]{2,0,1:T(8,128)(2,1)S(1)}, u32[]{:S(2)}, u32[]{:S(2)}) async-start(bf16[8,256,256]{2,0,1:T(8,128)(2,1)} %copy.74), calls=%async_computation | async-start | bytes 2097152 | tf_op jit(solution)/shard_map/all_to_all | solution.py:12
  134.7 0.0 all-gather.11.cloned.1.call-start
  134.8 0.7 all-gather.11.cloned.1.call-update
  135.5 0.1 reshape.57
  135.6 0.0 copy-start.2
  135.6 102.4 %all-gather.11.cloned.1.call-done = bf16[2,1024,256]{2,1,0:T(8,128)(2,1)} async-done(((bf16[2,64,256]{2,1,0:T(8,128)(2,1)}), bf16[2,1024,256]{2,1,0:T(8,128)(2,1)}) %all-gather.11.cloned.1.call-update) | async-done | bytes 1048592 | tf_op jit(solution)/shard_map/all_gather | solution.py:48
  238.0 1.7 convolution_convert_fusion.5
  239.7 1.6 copy.83
  241.2 16.7 %all-to-all-start.2 = ((bf16[8,256,256]{2,0,1:T(8,128)(2,1)}), bf16[8,256,256]{2,0,1:T(8,128)(2,1)}, u32[]{:S(2)}, u32[]{:S(2)}) async-start(bf16[8,256,256]{2,0,1:T(8,128)(2,1)} %copy.83), calls=%async_computation.2 | async-start | bytes 2097152 | tf_op jit(solution)/shard_map/all_to_all | solution.py:12
  257.9 0.0 all-gather.7.cloned.1.call-start
  258.0 0.7 all-gather.7.cloned.1.call-update
  258.7 0.0 all-gather.9.cloned.1.call-start
  258.7 0.5 all-gather.9.cloned.1.call-update
  259.2 0.3 copy.76
  259.6 26.5 %all-to-all-done.2 = bf16[8,256,256]{2,0,1:T(8,128)(2,1)} async-done(((bf16[8,256,256]{2,0,1:T(8,128)(2,1)}), bf16[8,256,256]{2,0,1:T(8,128)(2,1)}, u32[]{:S(2)}, u32[]{:S(2)}) %all-to-all-start.2) | async-done | bytes 1048608 | tf_op jit(solution)/shard_map/all_to_all | solution.py:12
  286.0 2.5 copy.85
  288.6 72.4 %all-gather.7.cloned.1.call-done = bf16[8,256,256]{2,1,0:T(8,128)(2,1)} async-done(((bf16[8,16,256]{2,1,0:T(8,128)(2,1)}), bf16[8,256,256]{2,1,0:T(8,128)(2,1)}) %all-gather.7.cloned.1.call-update) | async-done | bytes 1048592 | tf_op jit(solution)/shard_map/all_gather | solution.py:46
  361.0 3.1 fusion.17
  364.1 97.4 %all-gather.9.cloned.1.call-done = bf16[8,256,256]{2,1,0:T(8,128)(2,1)} async-done(((bf16[8,16,256]{2,1,0:T(8,128)(2,1)}), bf16[8,256,256]{2,1,0:T(8,128)(2,1)}) %all-gather.9.cloned.1.call-update) | async-done | bytes 1048592 | tf_op jit(solution)/shard_map/all_gather | solution.py:47
  461.5 4.0 fusion.6
  465.5 1.4 fusion.12
  467.0 2.7 copy.87
  469.7 17.5 %all-to-all-start.3 = ((bf16[8,256,256]{2,0,1:T(8,128)(2,1)}), bf16[8,256,256]{2,0,1:T(8,128)(2,1)}, u32[]{:S(2)}, u32[]{:S(2)}) async-start(bf16[8,256,256]{2,0,1:T(8,128)(2,1)} %copy.87), calls=%async_computation.3 | async-start | bytes 2097152 | tf_op jit(solution)/shard_map/all_to_all | solution.py:12
  487.2 0.0 reduce-scatter.7.cloned.1.call-start
  487.3 1.4 convolution_convert_fusion.2
  488.7 0.0 reduce-scatter.7.cloned.1.call-update
  488.7 2.7 fusion.11
  491.4 1.8 copy.78
  493.2 25.6 %all-to-all-done.3 = bf16[8,256,256]{2,0,1:T(8,128)(2,1)} async-done(((bf16[8,256,256]{2,0,1:T(8,128)(2,1)}), bf16[8,256,256]{2,0,1:T(8,128)(2,1)}, u32[]{:S(2)}, u32[]{:S(2)}) %all-to-all-start.3) | async-done | bytes 1048608 | tf_op jit(solution)/shard_map/all_to_all | solution.py:12
  518.9 21.3 %all-to-all-start.1 = ((bf16[8,256,256]{2,0,1:T(8,128)(2,1)}), bf16[8,256,256]{2,0,1:T(8,128)(2,1)S(1)}, u32[]{:S(2)}, u32[]{:S(2)}) async-start(bf16[8,256,256]{2,0,1:T(8,128)(2,1)} %copy.78), calls=%async_computation.1 | async-start | bytes 2097152 | tf_op jit(solution)/shard_map/all_to_all | solution.py:12
  540.2 0.0 reduce-scatter.9.cloned.1.call-start
  540.3 3.7 convolution_convert_fusion.1
  543.9 0.0 reduce-scatter.9.cloned.1.call-update
  544.0 0.2 reduce-scatter.5.cloned.1.call-start
  544.2 1.3 copy.89
  545.5 1.4 convolution_convert_fusion.3
  546.9 2.3 copy.92
  549.2 0.0 reduce-scatter.5.cloned.1.call-update
  549.2 0.0 reduce-scatter.11.cloned.1.call-start
  549.3 25.5 %all-to-all-done.1 = bf16[8,256,256]{2,0,1:T(8,128)(2,1)S(1)} async-done(((bf16[8,256,256]{2,0,1:T(8,128)(2,1)}), bf16[8,256,256]{2,0,1:T(8,128)(2,1)S(1)}, u32[]{:S(2)}, u32[]{:S(2)}) %all-to-all-start.1) | async-done | bytes 1048608 | tf_op jit(solution)/shard_map/all_to_all | solution.py:12
  574.8 1.0 copy-done
  575.7 1.3 copy.80
  577.0 1.4 convolution_convert_fusion
  578.4 0.0 reduce-scatter.11.cloned.1.call-update
  578.5 37.8 %reduce-scatter.7.cloned.1.call-done = bf16[8,16,256]{2,1,0:T(8,128)(2,1)} async-done(((bf16[8,256,256]{2,1,0:T(8,128)(2,1)}), bf16[8,16,256]{2,1,0:T(8,128)(2,1)}) %reduce-scatter.7.cloned.1.call-update) | async-done | bytes 65552 | tf_op jit(solution)/shard_map/reduce_scatter | solution.py:87
  616.2 1.5 convert_element_type.89
  617.8 106.2 %reduce-scatter.9.cloned.1.call-done = bf16[8,16,256]{2,1,0:T(8,128)(2,1)} async-done(((bf16[8,256,256]{2,1,0:T(8,128)(2,1)}), bf16[8,16,256]{2,1,0:T(8,128)(2,1)}) %reduce-scatter.9.cloned.1.call-update) | async-done | bytes 65552 | tf_op jit(solution)/shard_map/reduce_scatter | solution.py:90
  723.9 1.5 convert_element_type.91
  725.5 1.7 fusion.13
  727.2 0.8 copy.98
  728.0 0.5 fusion.14
  728.6 0.8 copy.99
  729.4 98.0 %reduce-scatter.5.cloned.1.call-done = bf16[2,16,1024]{2,1,0:T(8,128)(2,1)} async-done(((bf16[2,256,1024]{2,1,0:T(8,128)(2,1)}), bf16[2,16,1024]{2,1,0:T(8,128)(2,1)}) %reduce-scatter.5.cloned.1.call-update) | async-done | bytes 65552 | tf_op jit(solution)/shard_map/reduce_scatter | solution.py:84
  827.4 1.5 convert_element_type.87
  829.0 102.2 %reduce-scatter.11.cloned.1.call-done = bf16[2,64,256]{2,1,0:T(8,128)(2,1)} async-done(((bf16[2,1024,256]{2,1,0:T(8,128)(2,1)}), bf16[2,64,256]{2,1,0:T(8,128)(2,1)}) %reduce-scatter.11.cloned.1.call-update) | async-done | bytes 65552 | tf_op jit(solution)/shard_map/reduce_scatter | solution.py:93
  931.1 1.5 convert_element_type.95
  (10 shorter events, 0.0 us)
Async XLA Ops:
  7.2 105.7 %all-gather.5.cloned.1.call-start = ((), (), s32[]{:S(2)}) async-start(), calls=%async_computation.8 | async-start | bytes 1114112 | tf_op jit(solution)/shard_map/all_gather | solution.py:45
  114.8 20.7 %copy-start.5 = (bf16[256,512]{1,0:T(8,128)(2,1)S(1)}, bf16[256,512]{1,0:T(8,128)(2,1)}, u32[]{:S(2)}) copy-start(bf16[256,512]{1,0:T(8,128)(2,1)} %param.11) | copy-start | bytes 786436
  116.4 124.8 %all-to-all-start = ((bf16[8,256,256]{2,0,1:T(8,128)(2,1)}), bf16[8,256,256]{2,0,1:T(8,128)(2,1)S(1)}, u32[]{:S(2)}, u32[]{:S(2)}) async-start(bf16[8,256,256]{2,0,1:T(8,128)(2,1)} %copy.74), calls=%async_computation | async-start | bytes 2097152 | tf_op jit(solution)/shard_map/all_to_all | solution.py:12
  134.7 103.2 %all-gather.11.cloned.1.call-start = ((), (), s32[]{:S(2)}) async-start(), calls=%async_computation.11 | async-start | bytes 1114112 | tf_op jit(solution)/shard_map/all_gather | solution.py:48
  135.6 105.7 %copy-start.2 = (bf16[256,2,256]{2,1,0:T(2,128)(2,1)}, bf16[256,2,256]{2,1,0:T(2,128)(2,1)S(1)}, u32[]{:S(2)}) copy-start(bf16[256,2,256]{2,1,0:T(2,128)(2,1)S(1)} %reshape.57) | copy-start | bytes 786436
  241.2 44.8 %all-to-all-start.2 = ((bf16[8,256,256]{2,0,1:T(8,128)(2,1)}), bf16[8,256,256]{2,0,1:T(8,128)(2,1)}, u32[]{:S(2)}, u32[]{:S(2)}) async-start(bf16[8,256,256]{2,0,1:T(8,128)(2,1)} %copy.83), calls=%async_computation.2 | async-start | bytes 2097152 | tf_op jit(solution)/shard_map/all_to_all | solution.py:12
  257.9 103.1 %all-gather.7.cloned.1.call-start = ((), (), s32[]{:S(2)}) async-start(), calls=%async_computation.9 | async-start | bytes 1114112 | tf_op jit(solution)/shard_map/all_gather | solution.py:46
  258.7 202.8 %all-gather.9.cloned.1.call-start = ((), (), s32[]{:S(2)}) async-start(), calls=%async_computation.10 | async-start | bytes 1114112 | tf_op jit(solution)/shard_map/all_gather | solution.py:47
  461.5 4.0 copy-start.1
  469.7 49.2 %all-to-all-start.3 = ((bf16[8,256,256]{2,0,1:T(8,128)(2,1)}), bf16[8,256,256]{2,0,1:T(8,128)(2,1)}, u32[]{:S(2)}, u32[]{:S(2)}) async-start(bf16[8,256,256]{2,0,1:T(8,128)(2,1)} %copy.87), calls=%async_computation.3 | async-start | bytes 2097152 | tf_op jit(solution)/shard_map/all_to_all | solution.py:12
  487.2 129.0 %reduce-scatter.7.cloned.1.call-start = ((), (), s32[]{:S(2)}) async-start(), calls=%async_computation.13 | async-start | bytes 1114112 | tf_op jit(solution)/shard_map/reduce_scatter | solution.py:87
  491.4 48.8 %copy-start.4 = (bf16[32,8,8,256]{3,2,1,0:T(8,128)(2,1)S(1)}, bf16[32,8,8,256]{3,2,1,0:T(8,128)(2,1)}, u32[]{:S(2)}) copy-start(bf16[32,8,8,256]{3,2,1,0:T(8,128)(2,1)} %copy.85) | copy-start | bytes 3145732
  518.9 55.9 %all-to-all-start.1 = ((bf16[8,256,256]{2,0,1:T(8,128)(2,1)}), bf16[8,256,256]{2,0,1:T(8,128)(2,1)S(1)}, u32[]{:S(2)}, u32[]{:S(2)}) async-start(bf16[8,256,256]{2,0,1:T(8,128)(2,1)} %copy.78), calls=%async_computation.1 | async-start | bytes 2097152 | tf_op jit(solution)/shard_map/all_to_all | solution.py:12
  540.2 183.7 %reduce-scatter.9.cloned.1.call-start = ((), (), s32[]{:S(2)}) async-start(), calls=%async_computation.14 | async-start | bytes 1114112 | tf_op jit(solution)/shard_map/reduce_scatter | solution.py:90
  544.0 283.5 %reduce-scatter.5.cloned.1.call-start = ((), (), s32[]{:S(2)}) async-start(), calls=%async_computation.12 | async-start | bytes 1114112 | tf_op jit(solution)/shard_map/reduce_scatter | solution.py:84
  549.2 27.8 %copy-start.3 = (bf16[256,2,256]{2,1,0:T(2,128)(2,1)S(1)}, bf16[256,2,256]{2,1,0:T(2,128)(2,1)}, u32[]{:S(2)}) copy-start(bf16[256,2,256]{2,1,0:T(2,128)(2,1)} %copy-done.2) | copy-start | bytes 786436
  549.2 381.9 %reduce-scatter.11.cloned.1.call-start = ((), (), s32[]{:S(2)}) async-start(), calls=%async_computation.15 | async-start | bytes 1114112 | tf_op jit(solution)/shard_map/reduce_scatter | solution.py:93
  574.8 1.0 copy-start
Sparse Core Ops, SparseCore 0:
  10.1 102.7 all-gather.4
  137.6 100.2 all-gather.10
  260.8 100.1 all-gather.6
  363.0 98.5 all-gather.8
  490.5 125.6 reduce-scatter.6
  618.9 104.9 reduce-scatter.8
  726.8 100.6 reduce-scatter.4
  830.2 100.8 reduce-scatter.10
where the time goes:
time: 941 us; the launch traced here: 939 us
  waiting for transfers between devices  801 us (85%)
  starting transfers between devices  74.4 us (8%)
  matrix products  23.5 us (2%)
  local copies, waits for them, and re-layouts  20.6 us (2%)
  between operations  14.3 us (2%)
    reduce_scatter x1, waiting for transfers between devices, local(): lax.psum_scatter(grad_lower_right.astype(jnp.bfloat16), 'dp', scatter_dim...  106 us
    all_gather x1, waiting for transfers between devices, local(): lax.all_gather(upper_left, 'dp', axis=1, tiled=True)  104 us
    all_gather x1, waiting for transfers between devices, local(): lax.all_gather(lower_left, 'dp', axis=1, tiled=True)  102 us
    reduce_scatter x1, waiting for transfers between devices, local(): lax.psum_scatter(grad_lower_left.astype(jnp.bfloat16), 'dp', scatter_dime...  102 us
    reduce_scatter x1, waiting for transfers between devices, local(): lax.psum_scatter(grad_upper_left.astype(jnp.bfloat16), 'dp', scatter_dime...  98 us
    all_gather x1, waiting for transfers between devices, local(): lax.all_gather(lower_right, 'dp', axis=1, tiled=True)  97.4 us
    all_to_all x4, waiting for transfers between devices, permute(): lax.all_to_all(values, 'block', split_axis=1, concat_axis=0, tiled=True)  77.6 us
    all_to_all x4, starting transfers between devices, permute(): lax.all_to_all(values, 'block', split_axis=1, concat_axis=0, tiled=True)  73.9 us
  transfers between devices with their start and end apart: 12, of which 11 were waited for; matrix products, arithmetic and copies ran while one was open for 4% of the time, Pallas kernels for 0%

commit v1 on v0

--- a/solution.py
+++ b/solution.py
@@ -43,7 +43,9 @@
 def local(tokens, upper_left, upper_right, lower_right, lower_left, cotangent):
     weights = (
         lax.all_gather(upper_left, "dp", axis=1, tiled=True),
-        lax.all_gather(upper_right, "dp", axis=1, tiled=True),
+        jnp.concatenate(
+            lax.all_to_all(jnp.stack([upper_right] * lax.axis_size("dp")), "dp", 0, 0), axis=1
+        ),
         lax.all_gather(lower_right, "dp", axis=1, tiled=True),
         lax.all_gather(lower_left, "dp", axis=1, tiled=True),
     )

time: 941 us -> 850 us (0.903)
  waiting for transfers between devices: 801 us -> 695 us
  starting transfers between devices: 74.4 us -> 85.8 us
    all_gather x1 -> x0, waiting for transfers between devices: 72.4 us -> none  [local(): lax.all_gather(upper_right, 'dp', axis=1, tiled=True)]
    all_gather x1, waiting for transfers between devices: 97.4 us -> 71 us  [local(): lax.all_gather(lower_right, 'dp', axis=1, tiled=True)]
    all_to_all x0 -> x1, starting transfers between devices: none -> 12.6 us  [local(): lax.all_to_all(jnp.stack([upper_right] * lax.axis_size('dp')), 'dp', 0, 0)]
  transfers between devices with their start and end apart: 12 -> 12, of which waited for: 11 -> 10; matrix products, arithmetic and copies ran while one was open for 4% -> 5% of each run, Pallas kernels for 0% -> 0%
where the time goes in v1:
time: 850 us; the launch traced here: 849 us
  waiting for transfers between devices  695 us (82%)
  starting transfers between devices  85.8 us (10%)
  local copies, waits for them, and re-layouts  25.4 us (3%)
  matrix products  22.2 us (3%)
  between operations  14.3 us (2%)
    reduce_scatter x1, waiting for transfers between devices, local(): lax.psum_scatter(grad_lower_right.astype(jnp.bfloat16), 'dp', scatter_dim...  105 us
    reduce_scatter x1, waiting for transfers between devices, local(): lax.psum_scatter(grad_lower_left.astype(jnp.bfloat16), 'dp', scatter_dime...  102 us
    all_gather x1, waiting for transfers between devices, local(): lax.all_gather(lower_left, 'dp', axis=1, tiled=True)  101 us
    all_gather x1, waiting for transfers between devices, local(): lax.all_gather(upper_left, 'dp', axis=1, tiled=True)  99.6 us
    reduce_scatter x1, waiting for transfers between devices, local(): lax.psum_scatter(grad_upper_left.astype(jnp.bfloat16), 'dp', scatter_dime...  97.9 us
    all_to_all x4, waiting for transfers between devices, permute(): lax.all_to_all(values, 'block', split_axis=1, concat_axis=0, tiled=True)  76.8 us
    all_to_all x4, starting transfers between devices, permute(): lax.all_to_all(values, 'block', split_axis=1, concat_axis=0, tiled=True)  72.7 us
    all_gather x1, waiting for transfers between devices, local(): lax.all_gather(lower_right, 'dp', axis=1, tiled=True)  71 us
  transfers between devices with their start and end apart: 12, of which 10 were waited for; matrix products, arithmetic and copies ran while one was open for 5% of the time, Pallas kernels for 0%

profile of v1, /device:TPU:6, one launch (start us, length us, event | category | flops | bytes accessed | tf_op | source)
XLA Modules:
  0.0 848.9 jit_solution(16480845466362094097)
XLA Ops:
  7.2 2.0 stack.2
  9.2 12.6 %all-to-all-start.1 = ((bf16[16,8,16,256]{3,2,1,0:T(8,128)(2,1)}), bf16[16,8,16,256]{3,2,1,0:T(8,128)(2,1)S(1)}, u32[]{:S(2)}, u32[]{:S(2)}) async-start(bf16[16,8,16,256]{3,2,1,0:T(8,128)(2,1)} %stack.2), calls=%async_computation.1 | async-start | bytes 2097152 | tf_op jit(solution)/shard_map/all_to_all | solution.py:47
  21.8 0.0 all-gather.4.cloned.1.call-start
  21.9 0.7 all-gather.4.cloned.1.call-update
  22.6 0.1 reshape.60
  22.6 99.6 %all-gather.4.cloned.1.call-done = bf16[2,256,1024]{2,1,0:T(8,128)(2,1)} async-done(((bf16[2,16,1024]{2,1,0:T(8,128)(2,1)}), bf16[2,256,1024]{2,1,0:T(8,128)(2,1)}) %all-gather.4.cloned.1.call-update) | async-done | bytes 1048592 | tf_op jit(solution)/shard_map/all_gather | solution.py:45
  122.3 1.5 copy.72
  123.8 0.5 convolution_convert_fusion.7
  124.2 1.5 copy.74
  125.8 18.9 %all-to-all-start = ((bf16[8,256,256]{2,0,1:T(8,128)(2,1)}), bf16[8,256,256]{2,0,1:T(8,128)(2,1)S(1)}, u32[]{:S(2)}, u32[]{:S(2)}) async-start(bf16[8,256,256]{2,0,1:T(8,128)(2,1)} %copy.74), calls=%async_computation | async-start | bytes 2097152 | tf_op jit(solution)/shard_map/all_to_all | solution.py:12
  144.7 0.0 all-gather.8.cloned.1.call-start
  144.7 0.7 all-gather.8.cloned.1.call-update
  145.4 1.7 reshape.67
  147.2 100.8 %all-gather.8.cloned.1.call-done = bf16[2,1024,256]{2,1,0:T(8,128)(2,1)} async-done(((bf16[2,64,256]{2,1,0:T(8,128)(2,1)}), bf16[2,1024,256]{2,1,0:T(8,128)(2,1)}) %all-gather.8.cloned.1.call-update) | async-done | bytes 1048592 | tf_op jit(solution)/shard_map/all_gather | solution.py:50
  248.0 1.7 convolution_convert_fusion.5
  249.7 1.5 copy.84
  251.2 16.9 %all-to-all-start.3 = ((bf16[8,256,256]{2,0,1:T(8,128)(2,1)}), bf16[8,256,256]{2,0,1:T(8,128)(2,1)}, u32[]{:S(2)}, u32[]{:S(2)}) async-start(bf16[8,256,256]{2,0,1:T(8,128)(2,1)} %copy.84), calls=%async_computation.3 | async-start | bytes 2097152 | tf_op jit(solution)/shard_map/all_to_all | solution.py:12
  268.2 0.0 all-gather.6.cloned.1.call-start
  268.2 0.7 all-gather.6.cloned.1.call-update
  268.9 0.1 copy.77
  269.0 1.1 copy-done.4
  270.1 0.3 copy.76
  270.4 25.6 %all-to-all-done.3 = bf16[8,256,256]{2,0,1:T(8,128)(2,1)} async-done(((bf16[8,256,256]{2,0,1:T(8,128)(2,1)}), bf16[8,256,256]{2,0,1:T(8,128)(2,1)}, u32[]{:S(2)}, u32[]{:S(2)}) %all-to-all-start.3) | async-done | bytes 1048608 | tf_op jit(solution)/shard_map/all_to_all | solution.py:12
  296.0 2.5 copy.86
  298.5 1.8 fusion.17
  300.4 71.0 %all-gather.6.cloned.1.call-done = bf16[8,256,256]{2,1,0:T(8,128)(2,1)} async-done(((bf16[8,16,256]{2,1,0:T(8,128)(2,1)}), bf16[8,256,256]{2,1,0:T(8,128)(2,1)}) %all-gather.6.cloned.1.call-update) | async-done | bytes 1048592 | tf_op jit(solution)/shard_map/all_gather | solution.py:49
  371.4 3.9 fusion.6
  375.4 0.9 copy-done
  376.3 1.4 fusion.12
  377.8 2.7 copy.88
  380.5 16.2 %all-to-all-start.4 = ((bf16[8,256,256]{2,0,1:T(8,128)(2,1)}), bf16[8,256,256]{2,0,1:T(8,128)(2,1)}, u32[]{:S(2)}, u32[]{:S(2)}) async-start(bf16[8,256,256]{2,0,1:T(8,128)(2,1)} %copy.88), calls=%async_computation.4 | async-start | bytes 2097152 | tf_op jit(solution)/shard_map/all_to_all | solution.py:12
  396.7 0.0 reduce-scatter.7.cloned.1.call-start
  396.8 1.4 convolution_convert_fusion.2
  398.2 0.0 reduce-scatter.7.cloned.1.call-update
  398.2 2.7 fusion.11
  400.9 1.9 copy.79
  402.7 26.2 %all-to-all-done.4 = bf16[8,256,256]{2,0,1:T(8,128)(2,1)} async-done(((bf16[8,256,256]{2,0,1:T(8,128)(2,1)}), bf16[8,256,256]{2,0,1:T(8,128)(2,1)}, u32[]{:S(2)}, u32[]{:S(2)}) %all-to-all-start.4) | async-done | bytes 1048608 | tf_op jit(solution)/shard_map/all_to_all | solution.py:12
  428.9 20.7 %all-to-all-start.2 = ((bf16[8,256,256]{2,0,1:T(8,128)(2,1)}), bf16[8,256,256]{2,0,1:T(8,128)(2,1)S(1)}, u32[]{:S(2)}, u32[]{:S(2)}) async-start(bf16[8,256,256]{2,0,1:T(8,128)(2,1)} %copy.79), calls=%async_computation.2 | async-start | bytes 2097152 | tf_op jit(solution)/shard_map/all_to_all | solution.py:12
  449.6 0.0 reduce-scatter.9.cloned.1.call-start
  449.7 3.7 convolution_convert_fusion.1
  453.3 0.0 reduce-scatter.9.cloned.1.call-update
  453.4 0.2 reduce-scatter.5.cloned.1.call-start
  453.6 1.3 copy.90
  454.9 1.4 convolution_convert_fusion.3
  456.3 2.3 copy.93
  458.5 0.0 reduce-scatter.5.cloned.1.call-update
  458.6 0.0 reduce-scatter.11.cloned.1.call-start
  458.6 25.0 %all-to-all-done.2 = bf16[8,256,256]{2,0,1:T(8,128)(2,1)S(1)} async-done(((bf16[8,256,256]{2,0,1:T(8,128)(2,1)}), bf16[8,256,256]{2,0,1:T(8,128)(2,1)S(1)}, u32[]{:S(2)}, u32[]{:S(2)}) %all-to-all-start.2) | async-done | bytes 1048608 | tf_op jit(solution)/shard_map/all_to_all | solution.py:12
  483.6 0.9 copy-done.2
  484.6 1.3 copy.81
  485.9 1.4 convolution_convert_fusion
  487.3 0.0 reduce-scatter.11.cloned.1.call-update
  487.3 39.6 %reduce-scatter.7.cloned.1.call-done = bf16[8,16,256]{2,1,0:T(8,128)(2,1)} async-done(((bf16[8,256,256]{2,1,0:T(8,128)(2,1)}), bf16[8,16,256]{2,1,0:T(8,128)(2,1)}) %reduce-scatter.7.cloned.1.call-update) | async-done | bytes 65552 | tf_op jit(solution)/shard_map/reduce_scatter | solution.py:89
  526.9 1.5 convert_element_type.89
  528.4 105.1 %reduce-scatter.9.cloned.1.call-done = bf16[8,16,256]{2,1,0:T(8,128)(2,1)} async-done(((bf16[8,256,256]{2,1,0:T(8,128)(2,1)}), bf16[8,16,256]{2,1,0:T(8,128)(2,1)}) %reduce-scatter.9.cloned.1.call-update) | async-done | bytes 65552 | tf_op jit(solution)/shard_map/reduce_scatter | solution.py:92
  633.5 1.5 convert_element_type.91
  635.0 1.7 fusion.13
  636.7 0.8 copy.99
  637.6 0.5 fusion.14
  638.1 0.8 copy.100
  639.0 97.9 %reduce-scatter.5.cloned.1.call-done = bf16[2,16,1024]{2,1,0:T(8,128)(2,1)} async-done(((bf16[2,256,1024]{2,1,0:T(8,128)(2,1)}), bf16[2,16,1024]{2,1,0:T(8,128)(2,1)}) %reduce-scatter.5.cloned.1.call-update) | async-done | bytes 65552 | tf_op jit(solution)/shard_map/reduce_scatter | solution.py:86
  736.9 1.5 convert_element_type.87
  738.4 102.1 %reduce-scatter.11.cloned.1.call-done = bf16[2,64,256]{2,1,0:T(8,128)(2,1)} async-done(((bf16[2,1024,256]{2,1,0:T(8,128)(2,1)}), bf16[2,64,256]{2,1,0:T(8,128)(2,1)}) %reduce-scatter.11.cloned.1.call-update) | async-done | bytes 65552 | tf_op jit(solution)/shard_map/reduce_scatter | solution.py:95
  840.5 1.5 convert_element_type.95
  (15 shorter events, 0.0 us)
Async XLA Ops:
  7.2 15.4 %copy-start.7 = (bf16[256,512]{1,0:T(8,128)(2,1)S(1)}, bf16[256,512]{1,0:T(8,128)(2,1)}, u32[]{:S(2)}) copy-start(bf16[256,512]{1,0:T(8,128)(2,1)} %param.6) | copy-start | bytes 786436
  9.2 116.6 %all-to-all-start.1 = ((bf16[16,8,16,256]{3,2,1,0:T(8,128)(2,1)}), bf16[16,8,16,256]{3,2,1,0:T(8,128)(2,1)S(1)}, u32[]{:S(2)}, u32[]{:S(2)}) async-start(bf16[16,8,16,256]{3,2,1,0:T(8,128)(2,1)} %stack.2), calls=%async_computation.1 | async-start | bytes 2097152 | tf_op jit(solution)/shard_map/all_to_all | solution.py:47
  21.8 100.5 %all-gather.4.cloned.1.call-start = ((), (), s32[]{:S(2)}) async-start(), calls=%async_computation.9 | async-start | bytes 1114112 | tf_op jit(solution)/shard_map/all_gather | solution.py:45
  125.8 125.5 %all-to-all-start = ((bf16[8,256,256]{2,0,1:T(8,128)(2,1)}), bf16[8,256,256]{2,0,1:T(8,128)(2,1)S(1)}, u32[]{:S(2)}, u32[]{:S(2)}) async-start(bf16[8,256,256]{2,0,1:T(8,128)(2,1)} %copy.74), calls=%async_computation | async-start | bytes 2097152 | tf_op jit(solution)/shard_map/all_to_all | solution.py:12
  144.7 103.3 %all-gather.8.cloned.1.call-start = ((), (), s32[]{:S(2)}) async-start(), calls=%async_computation.11 | async-start | bytes 1114112 | tf_op jit(solution)/shard_map/all_gather | solution.py:50
  251.2 17.7 %copy-start.3 = (bf16[8,256,256]{2,0,1:T(8,128)(2,1)}, bf16[8,256,256]{2,0,1:T(8,128)(2,1)S(1)}, u32[]{:S(2)}) copy-start(bf16[8,256,256]{2,0,1:T(8,128)(2,1)S(1)} %all-to-all-done) | copy-start | bytes 3145732
  251.2 44.8 %all-to-all-start.3 = ((bf16[8,256,256]{2,0,1:T(8,128)(2,1)}), bf16[8,256,256]{2,0,1:T(8,128)(2,1)}, u32[]{:S(2)}, u32[]{:S(2)}) async-start(bf16[8,256,256]{2,0,1:T(8,128)(2,1)} %copy.84), calls=%async_computation.3 | async-start | bytes 2097152 | tf_op jit(solution)/shard_map/all_to_all | solution.py:12
  268.2 103.3 %all-gather.6.cloned.1.call-start = ((), (), s32[]{:S(2)}) async-start(), calls=%async_computation.10 | async-start | bytes 1114112 | tf_op jit(solution)/shard_map/all_gather | solution.py:49
  268.9 1.2 copy-start.4
  375.4 1.0 copy-start
  377.8 19.0 %copy-start.1 = (bf16[8,256,256]{1,2,0:T(8,128)(2,1)S(1)}, bf16[8,256,256]{1,2,0:T(8,128)(2,1)}, u32[]{:S(2)}) copy-start(bf16[8,256,256]{1,2,0:T(8,128)(2,1)} %copy-done) | copy-start | bytes 3145732
  380.5 48.4 %all-to-all-start.4 = ((bf16[8,256,256]{2,0,1:T(8,128)(2,1)}), bf16[8,256,256]{2,0,1:T(8,128)(2,1)}, u32[]{:S(2)}, u32[]{:S(2)}) async-start(bf16[8,256,256]{2,0,1:T(8,128)(2,1)} %copy.88), calls=%async_computation.4 | async-start | bytes 2097152 | tf_op jit(solution)/shard_map/all_to_all | solution.py:12
  396.7 130.2 %reduce-scatter.7.cloned.1.call-start = ((), (), s32[]{:S(2)}) async-start(), calls=%async_computation.13 | async-start | bytes 1114112 | tf_op jit(solution)/shard_map/reduce_scatter | solution.py:89
  400.9 48.8 %copy-start.6 = (bf16[32,8,8,256]{3,2,1,0:T(8,128)(2,1)S(1)}, bf16[32,8,8,256]{3,2,1,0:T(8,128)(2,1)}, u32[]{:S(2)}) copy-start(bf16[32,8,8,256]{3,2,1,0:T(8,128)(2,1)} %copy.86) | copy-start | bytes 3145732
  428.9 54.8 %all-to-all-start.2 = ((bf16[8,256,256]{2,0,1:T(8,128)(2,1)}), bf16[8,256,256]{2,0,1:T(8,128)(2,1)S(1)}, u32[]{:S(2)}, u32[]{:S(2)}) async-start(bf16[8,256,256]{2,0,1:T(8,128)(2,1)} %copy.79), calls=%async_computation.2 | async-start | bytes 2097152 | tf_op jit(solution)/shard_map/all_to_all | solution.py:12
  449.6 183.9 %reduce-scatter.9.cloned.1.call-start = ((), (), s32[]{:S(2)}) async-start(), calls=%async_computation.14 | async-start | bytes 1114112 | tf_op jit(solution)/shard_map/reduce_scatter | solution.py:92
  453.4 283.5 %reduce-scatter.5.cloned.1.call-start = ((), (), s32[]{:S(2)}) async-start(), calls=%async_computation.12 | async-start | bytes 1114112 | tf_op jit(solution)/shard_map/reduce_scatter | solution.py:86
  458.5 27.3 %copy-start.5 = (bf16[256,2,256]{2,1,0:T(2,128)(2,1)S(1)}, bf16[256,2,256]{2,1,0:T(2,128)(2,1)}, u32[]{:S(2)}) copy-start(bf16[256,2,256]{2,1,0:T(2,128)(2,1)} %reshape.67) | copy-start | bytes 786436
  458.6 382.0 %reduce-scatter.11.cloned.1.call-start = ((), (), s32[]{:S(2)}) async-start(), calls=%async_computation.15 | async-start | bytes 1114112 | tf_op jit(solution)/shard_map/reduce_scatter | solution.py:95
  483.6 0.9 copy-start.2
Sparse Core Ops, SparseCore 0:
  24.7 97.5 all-gather.3
  147.6 100.3 all-gather.7
  271.1 100.3 all-gather.5
  400.0 126.8 reduce-scatter.6
  529.6 103.8 reduce-scatter.8
  636.1 100.7 reduce-scatter.4
  739.7 100.7 reduce-scatter.10
